TPU v7x, 32 devices: a whole 2x2x4 slice. The times are simulated.
32 devices in a mesh: tp: 8 (over y, x, core), dp: 4 (over z).
Axes of the slice: x: 2, y: 2, z: 4, core: 2. Of those that a mesh axis runs over, the one named last changes fastest.
Arguments:
- grad_out: bfloat16 [512, 16384], P('dp', 'tp'), may hold values from -6 to 6
- hidden_sum: bfloat16 [512, 16384], P('dp', 'tp'), may hold values from -100 to 100
- norm_gain: float32 [16384], P('tp'), may hold values from 0.5 to 1.5
- out_weight: bfloat16 [2048, 16384], P(None, 'tp'), may hold values from -0.046875 to 0.046875
Outputs:
- resid_grad: bfloat16 [512, 16384], P('dp', 'tp')
- attn_grad: bfloat16 [512, 2048], P('dp', 'tp')
- gain_grad: float32 [16384], P('tp')
All inputs are finite; a program needn't handle non-finite values.
Results may differ from a plain program's by a relative error of at most 0.0049.
Values sent between devices are 32-bit elements; how exact they have to be, the bound alone decides.
No kernel may reach another device: no remote copies, remote signals or barrier semaphores. Data moves between devices by JAX's collectives and lax.ppermute only.
A program may use at most 64 MiB of HBM per device.

v0:
```python
import jax
import jax.numpy as jnp
from jax import lax
from jax.sharding import PartitionSpec as P

D = 16384


epsilon = 1e-05


def on_device(grad_out, hidden_sum, norm_gain, out_weight):
    upstream = grad_out.astype(jnp.float32)
    stream = hidden_sum.astype(jnp.float32)
    scaled = norm_gain * upstream
    squares = lax.psum(jnp.sum(stream * stream, axis=1), "tp")
    inverse = lax.rsqrt(squares / D + epsilon)
    normed = stream * inverse[:, None]
    dotted = lax.psum(jnp.sum(scaled * normed, axis=1), "tp")
    resid_full = inverse[:, None] * (scaled - normed * (dotted / D)[:, None])
    gain_grad = lax.psum(jnp.sum(upstream * normed, axis=0), "dp")
    resid_grad = resid_full.astype(jnp.bfloat16)
    partial_value = lax.dot_general(
        resid_grad, out_weight, (((1,), (1,)), ((), ())), preferred_element_type=jnp.float32
    )
    attn_grad = lax.psum_scatter(partial_value, "tp", scatter_dimension=1, tiled=True).astype(
        jnp.bfloat16
    )
    return (resid_grad, attn_grad, gain_grad)


def solution(mesh):
    return jax.shard_map(
        on_device,
        mesh=mesh,
        in_specs=(P("dp", "tp"), P("dp", "tp"), P("tp"), P(None, "tp")),
        out_specs=(P("dp", "tp"), P("dp", "tp"), P("tp")),
        check_vma=False,
    )
```

profile of v0, /device:TPU:0, one launch (start us, length us, event | category | flops | bytes accessed | tf_op | source)
XLA Modules:
  0.0 89.9 jit_solution(10686927400207809313)
XLA Ops:
  7.2 0.0 reduce-scatter.2.cloned.1.call-start
  7.2 1.2 %fusion.6 = f32[128]{0:T(128)S(1)} fusion(bf16[128,2048]{1,0:T(8,128)(2,1)} %param.5), kind=kLoop, calls=%fused_computation.10 | loop fusion | flops 786304 | bytes 524800 | tf_op jit(solution)/shard_map/reduce_sum | solution.py:16
  8.4 15.1 %psum.21 = f32[128]{0:T(128)S(1)} all-reduce(f32[128]{0:T(128)S(1)} %fusion.6), channel_id=1, replica_groups=mesh['tp'=8,'dp'=4] {'tp'}, use_global_device_ids=true, to_apply=%region_1.0 | all-reduce | flops 128 | bytes 1024 | tf_op jit(solution)/shard_map/psum | solution.py:16
  23.6 1.6 %fusion.7 = (f32[2048]{0:T(1024)S(1)}, f32[128]{0:T(128)S(1)}) fusion(bf16[128,2048]{1,0:T(8,128)(2,1)} %param.5, bf16[128,2048]{1,0:T(8,128)(2,1)} %param.4, f32[128]{0:T(128)S(1)} %add_rsqrt_fusion, f32[2048]{0:T(1024)} %param.6), kind=kLoop, calls=%fused_computation.11 | loop fusion | flops 2094976 | bytes 1065984 | tf_op jit(solution)/shard_map/reduce_sum | solution.py:21
  25.2 11.8 %psum.22 = f32[128]{0:T(128)S(1)} all-reduce(f32[128]{0:T(128)S(1)} %get-tuple-element.4), channel_id=1, replica_groups=mesh['tp'=8,'dp'=4] {'tp'}, use_global_device_ids=true, to_apply=%region_3.0 | all-reduce | flops 128 | bytes 1024 | tf_op jit(solution)/shard_map/psum | solution.py:19
  37.0 1.6 %fusion.4 = bf16[128,2048]{1,0:T(8,128)(2,1)S(1)} fusion(bf16[128,2048]{1,0:T(8,128)(2,1)} %param.4, bf16[128,2048]{1,0:T(8,128)(2,1)} %param.5, f32[128]{0:T(128)S(1)} %broadcast_multiply_fusion, f32[2048]{0:T(1024)} %param.6, f32[128]{0:T(128)S(1)} %add_rsqrt_fusion), kind=kLoop, calls=%fused_computation.8 | loop fusion | flops 2097152 | bytes 1582080 | tf_op jit(solution)/shard_map/convert_element_type | solution.py:22
  38.6 0.0 copy-start
  38.6 7.4 %fusion.8 = f32[128,2048]{1,0:T(8,128)} fusion(bf16[128,2048]{1,0:T(8,128)(2,1)S(1)} %fusion.4, bf16[2048,2048]{1,0:T(8,128)(2,1)} %param.7), kind=kOutput, calls=%fused_computation.14 | convolution fusion | flops 1073741824 | bytes 9961472 | tf_op jit(solution)/shard_map/dot_general | solution.py:23
  46.0 0.0 reduce-scatter.2.cloned.1.call-update
  46.1 12.8 %psum.23 = f32[2048]{0:T(1024)} all-reduce(f32[2048]{0:T(1024)S(1)} %get-tuple-element.3), channel_id=1, replica_groups=mesh['tp'=8,'dp'=4] {'dp'}, use_global_device_ids=true, to_apply=%region_6.0 | all-reduce | flops 2048 | bytes 16384 | tf_op jit(solution)/shard_map/psum | solution.py:21
  58.9 22.7 %reduce-scatter.2.cloned.1.call-done = f32[128,256]{1,0:T(8,128)} async-done(((f32[128,2048]{1,0:T(8,128)}), f32[128,256]{1,0:T(8,128)}) %reduce-scatter.2.cloned.1.call-update) | async-done | bytes 131088 | tf_op jit(solution)/shard_map/reduce_scatter | solution.py:26
  81.6 1.5 %convert_element_type.15 = bf16[128,256]{1,0:T(8,128)(2,1)} convert(f32[128,256]{1,0:T(8,128)} %reduce-scatter.2.cloned.1.call-done) | non-fusion elementwise | flops 32768 | bytes 196608 | tf_op jit(solution)/shard_map/convert_element_type | solution.py:26
  83.1 0.0 copy-done
  (2 shorter events, 0.0 us)
Async XLA Ops:
  7.2 74.4 %reduce-scatter.2.cloned.1.call-start = ((), (), s32[]{:S(2)}) async-start(), calls=%async_computation.1 | async-start | bytes 1179648 | tf_op jit(solution)/shard_map/reduce_scatter | solution.py:26
  38.6 44.5 %copy-start = (bf16[128,2048]{1,0:T(8,128)(2,1)}, bf16[128,2048]{1,0:T(8,128)(2,1)S(1)}, u32[]{:S(2)}) copy-start(bf16[128,2048]{1,0:T(8,128)(2,1)S(1)} %fusion.4) | copy-start | bytes 1572868
Sparse Core Ops, SparseCore 0:
  46.2 35.3 reduce-scatter.1
where the time goes:
time: 90.3 us; the launch traced here: 89.9 us
  blocking collectives  39.7 us (44%)
  waiting for transfers between devices  22.7 us (25%)
  between operations  14 us (16%)
  matrix products  7.44 us (8%)
  other arithmetic  5.98 us (7%)
    reduce_scatter x1, waiting for transfers between devices, on_device(): lax.psum_scatter(partial_value, 'tp', scatter_dimension=1, tiled=True)  22.7 us
    psum x1, blocking collectives, on_device(): squares = lax.psum(jnp.sum(stream * stream, axis=1), 'tp')  15.1 us
    psum x1, blocking collectives, on_device(): gain_grad = lax.psum(jnp.sum(upstream * normed, axis=0), 'dp')  12.8 us
    psum x1, blocking collectives, on_device(): dotted = lax.psum(jnp.sum(scaled * normed, axis=1), 'tp')  11.8 us
    dot_general x1, matrix products, on_device(): lax.dot_general(resid_grad, out_weight, (((1,), (1,)), ((), ())), preferr...  7.44 us
  transfers between devices with their start and end apart: 1, of which 1 were waited for; matrix products, arithmetic and copies ran while one was open for 0% of the time, Pallas kernels for 0%

commit v1 on v0

v1 whole, which is shorter than its diff:
```python
import jax
import jax.numpy as jnp
from jax import lax
from jax.experimental import pallas as pl
from jax.experimental.pallas import tpu as pltpu
from jax.sharding import PartitionSpec as P

epsilon = 1e-05
VMEM = 64 << 20
ROWS = 16
GROUP = 2
AHEAD = 4


def stats_kernel(go_hbm, hs_hbm, gain_hbm, st_ref, x, go, hs, gain, cols, sems):
    tokens, width = go.shape
    loads = [
        pltpu.make_async_copy(src, dst, sems.at[i])
        for i, (src, dst) in enumerate(((go_hbm, go), (hs_hbm, hs), (gain_hbm, gain)))
    ]
    for copy in loads:
        copy.start()
    for copy in loads:
        copy.wait()
    for t in range(0, tokens, ROWS):
        rows = pl.ds(t, ROWS)
        stream_b = hs[rows, :]
        stream = stream_b.astype(jnp.float32)
        scaled = gain[...] * go[rows, :].astype(jnp.float32)
        square = jnp.sum(stream * stream, axis=1, keepdims=True)
        dotted = jnp.sum(scaled * stream, axis=1, keepdims=True)
        factor = dotted / (square + epsilon * width)
        x[rows, :] = (scaled - stream * factor).astype(jnp.bfloat16)
        x[pl.ds(tokens + t, ROWS), :] = stream_b
        cols[0, rows, :] = square
        cols[1, rows, :] = dotted
        cols[2, rows, :] = factor
    diagonal = lax.broadcasted_iota(jnp.int32, (tokens, tokens), 0) == lax.broadcasted_iota(
        jnp.int32, (tokens, tokens), 1
    )
    for i in range(3):
        st_ref[i : i + 1, :] = jnp.sum(jnp.where(diagonal, cols[i], 0.0), axis=0, keepdims=True)


def local_stats(go, hs, gain):
    tokens, width = go.shape
    return pl.pallas_call(
        stats_kernel,
        out_shape=(pltpu.VMEM((3, tokens), jnp.float32), pltpu.VMEM((2 * tokens, width), jnp.bfloat16)),
        in_specs=[pl.BlockSpec(memory_space=pltpu.HBM)] * 3,
        out_specs=(pl.BlockSpec(memory_space=pltpu.VMEM),) * 2,
        scratch_shapes=[
            pltpu.VMEM((tokens, width), jnp.bfloat16),
            pltpu.VMEM((tokens, width), jnp.bfloat16),
            pltpu.VMEM((1, width), jnp.float32),
            pltpu.VMEM((3, tokens, 1), jnp.float32),
            pltpu.SemaphoreType.DMA((3,)),
        ],
        compiler_params=pltpu.CompilerParams(vmem_limit_bytes=VMEM - 4 * tokens * width - (3 << 17)),
        cost_estimate=pl.CostEstimate(flops=8 * tokens * width, bytes_accessed=4 * tokens * width, transcendentals=0),
    )(go, hs, gain.reshape(1, width))


def products_kernel(low_ref, st_ref, x, w_hbm, give_ref, keep_ref, w, sems):
    tokens = st_ref.shape[1]
    blocks, n, width = w.shape
    group = min(GROUP, blocks)
    low, half = low_ref[0], blocks // 2

    def load(j):
        source = 2 * (j % half) + (1 - low if j < half else low)
        return pltpu.make_async_copy(w_hbm.at[pl.ds(source * n, n), :], w.at[j], sems.at[j])

    loads = [load(j) for j in range(blocks)]
    for copy in loads[:AHEAD]:
        copy.start()
    for g in range(0, blocks, group):
        for j in range(g, g + group):
            loads[j].wait()
            if j + AHEAD < blocks:
                loads[j + AHEAD].start()
        both = lax.dot_general(
            w[g : g + group].reshape(group * n, width),
            x[...],
            (((1,), (1,)), ((), ())),
            preferred_element_type=jnp.float32,
        )
        for k in range(group):
            j = g + k
            part = both[k * n : (k + 1) * n]
            second = part[:, tokens:]
            out = give_ref if j < half else keep_ref
            out[0, j % half] = part[:, :tokens] + st_ref[2:3, :] * second
            out[1, j % half] = second


def products(low, stats, x, w, blocks):
    tokens = stats.shape[1]
    rows, width = w.shape
    n = rows // blocks
    vmem = pl.BlockSpec(memory_space=pltpu.VMEM)
    return pl.pallas_call(
        products_kernel,
        out_shape=(pltpu.VMEM((2, blocks // 2, n, tokens), jnp.float32),) * 2,
        in_specs=[pl.BlockSpec(memory_space=pltpu.SMEM), vmem, vmem, pl.BlockSpec(memory_space=pltpu.HBM)],
        out_specs=(vmem, vmem),
        scratch_shapes=[pltpu.VMEM((blocks, n, width), jnp.bfloat16), pltpu.SemaphoreType.DMA((blocks,))],
        compiler_params=pltpu.CompilerParams(vmem_limit_bytes=VMEM - 16 * tokens * rows // 2 - 4 * tokens * width - (3 << 20)),
        cost_estimate=pl.CostEstimate(
            flops=4 * tokens * rows * width, bytes_accessed=2 * rows * width, transcendentals=0
        ),
    )(low.reshape(1), stats, pltpu.with_memory_space_constraint(x, pltpu.VMEM), w)


def swap(value, axis, size, mask):
    return lax.ppermute(value, axis, [(i, i ^ mask(i)) for i in range(size)])


def build(tp, dp):
    count = tp.bit_length() - 2

    def order(i, step):
        return step if i & 1 == 0 else count - 1 - step

    def body(grad_out, hidden_sum, norm_gain, out_weight):
        features = grad_out.shape[1] * tp
        me = lax.axis_index("tp")
        low, upper = me & 1, me >> 1
        local, x = local_stats(grad_out, hidden_sum, norm_gain)
        stats = local[:2] + swap(local[:2], "tp", tp, lambda i: 1)
        local, x, stats = lax.optimization_barrier((local, x, stats))
        give, keep = products(low, local, x, out_weight, tp)
        for bit in range(1, count + 1):
            other = swap(stats, "tp", tp, lambda i: 1 << bit)
            stats = stats + other
        from_pair = swap(give, "tp", tp, lambda i: 1)
        inverse = lax.rsqrt(stats[0] / features + epsilon)
        factor = inverse * inverse * stats[1] / features

        pair = keep + from_pair
        partial = inverse * (pair[0] - factor * pair[1])

        def wanted(step, own):
            mine = jnp.where(low == 0, upper >> order(0, step), upper >> order(1, step)) & 1
            return mine if own else 1 - mine

        def blocks_of(step, bit):
            pieces = []
            for offset in range(1 << (count - step - 1)):
                def number(parity):
                    value = bit << order(parity, step)
                    for k, s in enumerate(range(step + 1, count)):
                        value = value | (((offset >> k) & 1) << order(parity, s))
                    return value

                which = jnp.where(low == 0, number(0), number(1))
                pieces.append(lax.dynamic_index_in_dim(partial, which, 0, True))
            return jnp.concatenate(pieces, 0) if len(pieces) > 1 else pieces[0]

        def halve(source, step, own):
            if step == 0:
                return blocks_of(step, wanted(step, own))
            shaped = source.reshape((-1, 2) + source.shape[1:])
            return lax.dynamic_index_in_dim(shaped, wanted(step, own), 1, False)

        current, sums = None, None
        for step in range(count):
            given = halve(current, step, False)
            if step == 1:
                given, sums = lax.optimization_barrier((given, sums))
            got = swap(given, "tp", tp, lambda i: 2 << order(i, step))
            if step == 0:
                upstream = grad_out.astype(jnp.float32)
                stream = hidden_sum.astype(jnp.float32)
                resid_grad = (
                    inverse[:, None] * (norm_gain * upstream - stream * factor[:, None])
                ).astype(jnp.bfloat16)
                sums = jnp.sum(upstream * stream * inverse[:, None], axis=0)
                if dp > 1:
                    sums = sums + swap(sums, "dp", dp, lambda i: 1)
            current = halve(current, step, True) + got
        attn_grad = current[0].T.astype(jnp.bfloat16)
        mask = 2
        while mask < dp:
            sums = sums + swap(sums, "dp", dp, lambda i: mask)
            mask *= 2
        return (resid_grad, attn_grad, sums)

    return body


def solution(mesh):
    return jax.shard_map(
        build(mesh.shape["tp"], mesh.shape["dp"]),
        mesh=mesh,
        in_specs=(P("dp", "tp"), P("dp", "tp"), P("tp"), P(None, "tp")),
        out_specs=(P("dp", "tp"), P("dp", "tp"), P("tp")),
        check_vma=False,
    )
```

time: 90.3 us -> 35.6 us (0.39)
  blocking collectives: 39.7 us -> 0 us
  waiting for transfers between devices: 22.7 us -> 7.96 us
  starting transfers between devices: 0.04 us -> 13.5 us
  between operations: 14 us -> 0.74 us
  Pallas kernels: 0 us -> 9.07 us
  matrix products: 7.44 us -> 0 us
  other arithmetic: 5.98 us -> 3.38 us
    psum x3 -> x0, blocking collectives: 39.7 us -> none  [the longest x1 15.1 us: on_device(): squares = lax.psum(jnp.sum(stream * stream, axis=1), 'tp')]
    reduce_scatter x1 -> x0, waiting for transfers between devices: 22.7 us -> none  [on_device(): lax.psum_scatter(partial_value, 'tp', scatter_dimension=1, tiled=True)]
    ppermute x0 -> x8, starting transfers between devices: none -> 13.5 us  [swap(): return lax.ppermute(value, axis, [(i, i ^ mask(i)) for i in range(size)])]
    pallas_call x0 -> x2, Pallas kernels: none -> 9.07 us  [the longest x1 7.36 us: products(): pl.pallas_call(products_kernel, out_shape=(pltpu.VMEM((2, blocks // 2, n,...]
    ppermute x0 -> x8, waiting for transfers between devices: none -> 7.96 us  [swap(): return lax.ppermute(value, axis, [(i, i ^ mask(i)) for i in range(size)])]
    dot_general x1 -> x0, matrix products: 7.44 us -> none  [on_device(): lax.dot_general(resid_grad, out_weight, (((1,), (1,)), ((), ())), preferr...]
    convert_element_type x2 -> x1, other arithmetic: 3.11 us -> 0.02 us  [body(): attn_grad = current[0].T.astype(jnp.bfloat16)]
    reduce_sum x2 -> x1, other arithmetic: 2.86 us -> 2.51 us  [body(): sums = jnp.sum(upstream * stream * inverse[:, None], axis=0)]
  transfers between devices with their start and end apart: 1 -> 8, of which waited for: 1 -> 5; matrix products, arithmetic and copies ran while one was open for 0% -> 9% of each run, Pallas kernels for 0% -> 0%
where the time goes in v1:
time: 35.6 us; the launch traced here: 35.4 us
  starting transfers between devices  13.5 us (38%)
  Pallas kernels  9.07 us (25%)
  waiting for transfers between devices  7.96 us (22%)
  other arithmetic  3.38 us (9%)
  local copies, waits for them, and re-layouts  0.82 us (2%)
  between operations  0.74 us (2%)
    ppermute x8, starting transfers between devices, swap(): return lax.ppermute(value, axis, [(i, i ^ mask(i)) for i in range(size)])  13.5 us
    ppermute x8, waiting for transfers between devices, swap(): return lax.ppermute(value, axis, [(i, i ^ mask(i)) for i in range(size)])  7.96 us
    pallas_call x1, Pallas kernels, products(): pl.pallas_call(products_kernel, out_shape=(pltpu.VMEM((2, blocks // 2, n,...  7.36 us
    reduce_sum x1, other arithmetic, body(): sums = jnp.sum(upstream * stream * inverse[:, None], axis=0)  2.51 us
    pallas_call x1, Pallas kernels, local_stats(): pl.pallas_call(stats_kernel, out_shape=(pltpu.VMEM((3, tokens), jnp.float...  1.71 us
    unnamed x5, local copies, waits for them, and re-layouts  0.75 us
  transfers between devices with their start and end apart: 8, of which 5 were waited for; matrix products, arithmetic and copies ran while one was open for 9% of the time, Pallas kernels for 0%

profile of v1, /device:TPU:0, one launch (start us, length us, event | category | flops | bytes accessed | tf_op | source)
XLA Modules:
  0.0 35.4 jit_solution(2825188955732159962)
XLA Ops:
  0.6 0.0 copy-start.1
  0.6 1.7 %shard_map.67 = (f32[3,128]{1,0:T(4,128)S(1)}, bf16[256,2048]{1,0:T(8,128)(2,1)S(1)}) custom-call(bf16[128,2048]{1,0:T(8,128)(2,1)} %go_hbm.1, bf16[128,2048]{1,0:T(8,128)(2,1)} %hs_hbm.1, f32[1,2048]{1,0:T(1,128)} %bitcast.26), custom_call_target="tpu_custom_call" | custom-call | flops 2097152 | bytes 1048576 | tf_op jit(solution)/shard_map/pallas_call | solution.py:47
  2.4 0.0 copy-start
  2.4 0.6 %collective-permute-start = (f32[2,128]{1,0:T(2,128)S(1)}, f32[2,128]{1,0:T(2,128)S(1)}, u32[]{:S(2)}, u32[]{:S(2)}) collective-permute-start(f32[2,128]{1,0:T(2,128)S(1)} %slice.16), channel_id=1, source_target_pairs={{0,4},{4,0},{8,12},{12,8},{16,20},{20,16},{24,28},{28,24},{1,5},{5... | collective-permute-start | bytes 3080 | tf_op jit(solution)/shard_map/ppermute | solution.py:116
  2.9 0.8 %collective-permute-done = f32[2,128]{1,0:T(2,128)S(1)} collective-permute-done((f32[2,128]{1,0:T(2,128)S(1)}, f32[2,128]{1,0:T(2,128)S(1)}, u32[]{:S(2)}, u32[]{:S(2)}) %collective-permute-start) | collective-permute-done | bytes 1056 | tf_op jit(solution)/shard_map/ppermute | solution.py:116
  3.8 0.0 copy-done
  3.8 7.4 %shard_map.68 = (f32[2,4,256,128]{3,2,1,0:T(8,128)S(1)}, f32[2,4,256,128]{3,2,1,0:T(8,128)S(1)}) custom-call(s32[1]{0:T(128)} %bitcast.3.low_ref, f32[3,128]{1,0:T(4,128)} %copy-done, bf16[256,2048]{1,0:T(8,128)(2,1)S(1)} %get-tuple-element.16.x, bf16[2048,2048]{1,0:T(8,128)(2,1)} %w_hbm.1), custom_call_target="tpu_custom_call" | custom-call | flops 2147483648 | bytes 8388608 | tf_op jit(solution)/shard_map/pallas_call | solution.py:102
  11.1 0.4 %collective-permute-start.3 = (f32[2,4,256,128]{3,2,1,0:T(8,128)S(1)}, f32[2,4,256,128]{3,2,1,0:T(8,128)S(1)}, u32[]{:S(2)}, u32[]{:S(2)}) collective-permute-start(f32[2,4,256,128]{3,2,1,0:T(8,128)S(1)} %get-tuple-element.18), channel_id=1, source_target_pairs={{0,4},{4,0},{8,12},{12,8},{16,20},{20,16},{24,28},{28,24},{1,5},{5... | collective-permute-start | bytes 3145736 | tf_op jit(solution)/shard_map/ppermute | solution.py:116
  11.5 2.6 %collective-permute-start.1 = (f32[2,128]{1,0:T(2,128)S(1)}, f32[2,128]{1,0:T(2,128)S(1)}, u32[]{:S(2)}, u32[]{:S(2)}) collective-permute-start(f32[2,128]{1,0:T(2,128)S(1)} %slice_add_fusion), channel_id=1, source_target_pairs={{0,8},{4,12},{8,0},{12,4},{16,24},{20,28},{24,16},{28,20},{1,9},{5... | collective-permute-start | bytes 3080 | tf_op jit(solution)/shard_map/ppermute | solution.py:116
  14.2 1.6 %collective-permute-done.1 = f32[2,128]{1,0:T(2,128)S(1)} collective-permute-done((f32[2,128]{1,0:T(2,128)S(1)}, f32[2,128]{1,0:T(2,128)S(1)}, u32[]{:S(2)}, u32[]{:S(2)}) %collective-permute-start.1) | collective-permute-done | bytes 1056 | tf_op jit(solution)/shard_map/ppermute | solution.py:116
  15.7 2.1 %collective-permute-start.2 = (f32[2,128]{1,0:T(2,128)S(1)}, f32[2,128]{1,0:T(2,128)S(1)}, u32[]{:S(2)}, u32[]{:S(2)}) collective-permute-start(f32[2,128]{1,0:T(2,128)S(1)} %add.67), channel_id=1, source_target_pairs={{0,16},{4,20},{8,24},{12,28},{16,0},{20,4},{24,8},{28,12},{1,17},{... | collective-permute-start | bytes 3080 | tf_op jit(solution)/shard_map/ppermute | solution.py:116
  17.8 1.6 %collective-permute-done.2 = f32[2,128]{1,0:T(2,128)S(1)} collective-permute-done((f32[2,128]{1,0:T(2,128)S(1)}, f32[2,128]{1,0:T(2,128)S(1)}, u32[]{:S(2)}, u32[]{:S(2)}) %collective-permute-start.2) | collective-permute-done | bytes 1056 | tf_op jit(solution)/shard_map/ppermute | solution.py:116
  19.4 0.0 collective-permute-done.3
  19.4 0.1 add.71
  19.5 0.1 fusion.7
  19.6 2.1 %collective-permute-start.4 = (f32[2,256,128]{2,1,0:T(8,128)S(1)}, f32[2,256,128]{2,1,0:T(8,128)S(1)}, u32[]{:S(2)}, u32[]{:S(2)}) collective-permute-start(f32[2,256,128]{2,1,0:T(8,128)S(1)} %pad_maximum_fusion), channel_id=1, source_target_pairs={{0,8},{4,20},{8,0},{12,28},{16,24},{20,4},{24,16},{28,12},{1,9},{5... | collective-permute-start | bytes 786440 | tf_op jit(solution)/shard_map/ppermute | solution.py:116
  21.7 0.0 copy-done.1
  21.7 2.5 %fusion.4 = (f32[2048]{0:T(1024)S(1)}, bf16[128,2048]{1,0:T(8,128)(2,1)}) fusion(bf16[128,2048]{1,0:T(8,128)(2,1)} %hs_hbm.1, bf16[128,2048]{1,0:T(8,128)(2,1)} %go_hbm.1, f32[128]{0:T(128)S(1)} %rsqrt_bitcast_fusion, f32[128]{0:T(128)S(1)} %fusion.9, f32[2048]{0:T(1024)S(1)} %copy-done.1), kind=kLoop, calls=%fused_computation.7 | loop fusion | flops 2619392 | bytes 1590272 | tf_op jit(solution)/shard_map/reduce_sum | solution.py:178
  24.2 1.6 %collective-permute-start.5 = (f32[2048]{0:T(1024)S(1)}, f32[2048]{0:T(1024)S(1)}, u32[]{:S(2)}, u32[]{:S(2)}) collective-permute-start(f32[2048]{0:T(1024)S(1)} %get-tuple-element.24), channel_id=1, source_target_pairs={{0,1},{1,0},{2,3},{3,2},{4,5},{5,4},{6,7},{7,6},{8,9},{9,8},{10,11... | collective-permute-start | bytes 24584 | tf_op jit(solution)/shard_map/ppermute | solution.py:116
  25.8 2.1 %collective-permute-done.5 = f32[2048]{0:T(1024)S(1)} collective-permute-done((f32[2048]{0:T(1024)S(1)}, f32[2048]{0:T(1024)S(1)}, u32[]{:S(2)}, u32[]{:S(2)}) %collective-permute-start.5) | collective-permute-done | bytes 8224 | tf_op jit(solution)/shard_map/ppermute | solution.py:116
  27.9 0.0 collective-permute-done.4
  27.9 1.6 %collective-permute-start.6 = (f32[1,256,128]{2,1,0:T(8,128)S(1)}, f32[1,256,128]{2,1,0:T(8,128)S(1)}, u32[]{:S(2)}, u32[]{:S(2)}) collective-permute-start(f32[1,256,128]{2,1,0:T(8,128)S(1)} %constant_dynamic-slice_fusion), channel_id=1, source_target_pairs={{0,16},{4,12},{8,24},{12,4},{16,0},{20,28},{24,8},{28,20},{1,17},{... | collective-permute-start | bytes 393224 | tf_op jit(solution)/shard_map/ppermute | solution.py:116
  29.5 2.6 %collective-permute-start.7 = (f32[2048]{0:T(1024)S(1)}, f32[2048]{0:T(1024)S(1)}, u32[]{:S(2)}, u32[]{:S(2)}) collective-permute-start(f32[2048]{0:T(1024)S(1)} %add.79), channel_id=1, source_target_pairs={{0,2},{1,3},{2,0},{3,1},{4,6},{5,7},{6,4},{7,5},{8,10},{9,11},{10,... | collective-permute-start | bytes 24584 | tf_op jit(solution)/shard_map/ppermute | solution.py:116
  32.1 2.0 %collective-permute-done.7 = f32[2048]{0:T(1024)S(1)} collective-permute-done((f32[2048]{0:T(1024)S(1)}, f32[2048]{0:T(1024)S(1)}, u32[]{:S(2)}, u32[]{:S(2)}) %collective-permute-start.7) | collective-permute-done | bytes 8224 | tf_op jit(solution)/shard_map/ppermute | solution.py:116
  34.1 0.6 %add.81 = f32[2048]{0:T(1024)} add(f32[2048]{0:T(1024)S(1)} %add.79, f32[2048]{0:T(1024)S(1)} %collective-permute-done.7) | non-fusion elementwise | flops 2048 | bytes 24576 | tf_op jit(solution)/shard_map/add | solution.py:185
  34.7 0.0 collective-permute-done.6
  34.7 0.7 %copy.7 = bf16[128,256]{1,0:T(8,128)(2,1)} copy(bf16[128,256]{0,1:T(8,128)(2,1)S(1)} %fusion.8) | data formatting | bytes 131072
  (12 shorter events, 0.2 us)
Async XLA Ops:
  0.6 21.1 %copy-start.1 = (f32[2048]{0:T(1024)S(1)}, f32[2048]{0:T(1024)}, u32[]{:S(2)}) copy-start(f32[2048]{0:T(1024)} %param.6) | copy-start | bytes 24580
  2.4 1.4 %copy-start = (f32[3,128]{1,0:T(4,128)}, f32[3,128]{1,0:T(4,128)S(1)}, u32[]{:S(2)}) copy-start(f32[3,128]{1,0:T(4,128)S(1)} %get-tuple-element.15.st_ref) | copy-start | bytes 4612
  2.4 1.4 %collective-permute-start = (f32[2,128]{1,0:T(2,128)S(1)}, f32[2,128]{1,0:T(2,128)S(1)}, u32[]{:S(2)}, u32[]{:S(2)}) collective-permute-start(f32[2,128]{1,0:T(2,128)S(1)} %slice.16), channel_id=1, source_target_pairs={{0,4},{4,0},{8,12},{12,8},{16,20},{20,16},{24,28},{28,24},{1,5},{5... | collective-permute-start | bytes 3080 | tf_op jit(solution)/shard_map/ppermute | solution.py:116
  11.1 8.2 %collective-permute-start.3 = (f32[2,4,256,128]{3,2,1,0:T(8,128)S(1)}, f32[2,4,256,128]{3,2,1,0:T(8,128)S(1)}, u32[]{:S(2)}, u32[]{:S(2)}) collective-permute-start(f32[2,4,256,128]{3,2,1,0:T(8,128)S(1)} %get-tuple-element.18), channel_id=1, source_target_pairs={{0,4},{4,0},{8,12},{12,8},{16,20},{20,16},{24,28},{28,24},{1,5},{5... | collective-permute-start | bytes 3145736 | tf_op jit(solution)/shard_map/ppermute | solution.py:116
  11.5 4.2 %collective-permute-start.1 = (f32[2,128]{1,0:T(2,128)S(1)}, f32[2,128]{1,0:T(2,128)S(1)}, u32[]{:S(2)}, u32[]{:S(2)}) collective-permute-start(f32[2,128]{1,0:T(2,128)S(1)} %slice_add_fusion), channel_id=1, source_target_pairs={{0,8},{4,12},{8,0},{12,4},{16,24},{20,28},{24,16},{28,20},{1,9},{5... | collective-permute-start | bytes 3080 | tf_op jit(solution)/shard_map/ppermute | solution.py:116
  15.7 3.6 %collective-permute-start.2 = (f32[2,128]{1,0:T(2,128)S(1)}, f32[2,128]{1,0:T(2,128)S(1)}, u32[]{:S(2)}, u32[]{:S(2)}) collective-permute-start(f32[2,128]{1,0:T(2,128)S(1)} %add.67), channel_id=1, source_target_pairs={{0,16},{4,20},{8,24},{12,28},{16,0},{20,4},{24,8},{28,12},{1,17},{... | collective-permute-start | bytes 3080 | tf_op jit(solution)/shard_map/ppermute | solution.py:116
  19.6 8.2 %collective-permute-start.4 = (f32[2,256,128]{2,1,0:T(8,128)S(1)}, f32[2,256,128]{2,1,0:T(8,128)S(1)}, u32[]{:S(2)}, u32[]{:S(2)}) collective-permute-start(f32[2,256,128]{2,1,0:T(8,128)S(1)} %pad_maximum_fusion), channel_id=1, source_target_pairs={{0,8},{4,20},{8,0},{12,28},{16,24},{20,4},{24,16},{28,12},{1,9},{5... | collective-permute-start | bytes 786440 | tf_op jit(solution)/shard_map/ppermute | solution.py:116
  24.2 3.7 %collective-permute-start.5 = (f32[2048]{0:T(1024)S(1)}, f32[2048]{0:T(1024)S(1)}, u32[]{:S(2)}, u32[]{:S(2)}) collective-permute-start(f32[2048]{0:T(1024)S(1)} %get-tuple-element.24), channel_id=1, source_target_pairs={{0,1},{1,0},{2,3},{3,2},{4,5},{5,4},{6,7},{7,6},{8,9},{9,8},{10,11... | collective-permute-start | bytes 24584 | tf_op jit(solution)/shard_map/ppermute | solution.py:116
  27.9 6.7 %collective-permute-start.6 = (f32[1,256,128]{2,1,0:T(8,128)S(1)}, f32[1,256,128]{2,1,0:T(8,128)S(1)}, u32[]{:S(2)}, u32[]{:S(2)}) collective-permute-start(f32[1,256,128]{2,1,0:T(8,128)S(1)} %constant_dynamic-slice_fusion), channel_id=1, source_target_pairs={{0,16},{4,12},{8,24},{12,4},{16,0},{20,28},{24,8},{28,20},{1,17},{... | collective-permute-start | bytes 393224 | tf_op jit(solution)/shard_map/ppermute | solution.py:116
  29.5 4.5 %collective-permute-start.7 = (f32[2048]{0:T(1024)S(1)}, f32[2048]{0:T(1024)S(1)}, u32[]{:S(2)}, u32[]{:S(2)}) collective-permute-start(f32[2048]{0:T(1024)S(1)} %add.79), channel_id=1, source_target_pairs={{0,2},{1,3},{2,0},{3,1},{4,6},{5,7},{6,4},{7,5},{8,10},{9,11},{10,... | collective-permute-start | bytes 24584 | tf_op jit(solution)/shard_map/ppermute | solution.py:116

commit v2 on v1

--- a/solution.py
+++ b/solution.py
@@ -1,3 +1,5 @@
+import functools
+
 import jax
 import jax.numpy as jnp
 from jax import lax
@@ -9,7 +11,6 @@
 VMEM = 64 << 20
 ROWS = 16
 GROUP = 2
-AHEAD = 4
 
 
 def stats_kernel(go_hbm, hs_hbm, gain_hbm, st_ref, x, go, hs, gain, cols, sems):
@@ -61,24 +62,21 @@
     )(go, hs, gain.reshape(1, width))
 
 
-def products_kernel(low_ref, st_ref, x, w_hbm, give_ref, keep_ref, w, sems):
+def products_kernel(flip, st_ref, x, w_hbm, out_ref, w, sems):
     tokens = st_ref.shape[1]
-    blocks, n, width = w.shape
-    group = min(GROUP, blocks)
-    low, half = low_ref[0], blocks // 2
+    half, n, width = w.shape
+    group = min(GROUP, half)
+    parity = (lax.axis_index("tp") + flip) % 2
 
     def load(j):
-        source = 2 * (j % half) + (1 - low if j < half else low)
-        return pltpu.make_async_copy(w_hbm.at[pl.ds(source * n, n), :], w.at[j], sems.at[j])
-
-    loads = [load(j) for j in range(blocks)]
-    for copy in loads[:AHEAD]:
+        return pltpu.make_async_copy(w_hbm.at[pl.ds((2 * j + parity) * n, n), :], w.at[j], sems.at[j])
+
+    loads = [load(j) for j in range(half)]
+    for copy in loads:
         copy.start()
-    for g in range(0, blocks, group):
+    for g in range(0, half, group):
         for j in range(g, g + group):
             loads[j].wait()
-            if j + AHEAD < blocks:
-                loads[j + AHEAD].start()
         both = lax.dot_general(
             w[g : g + group].reshape(group * n, width),
             x[...],
@@ -86,30 +84,32 @@
             preferred_element_type=jnp.float32,
         )
         for k in range(group):
-            j = g + k
             part = both[k * n : (k + 1) * n]
             second = part[:, tokens:]
-            out = give_ref if j < half else keep_ref
-            out[0, j % half] = part[:, :tokens] + st_ref[2:3, :] * second
-            out[1, j % half] = second
-
-
-def products(low, stats, x, w, blocks):
+            out_ref[0, g + k] = part[:, :tokens] + st_ref[2:3, :] * second
+            out_ref[1, g + k] = second
+
+
+def products(flip, stats, x, w, blocks):
     tokens = stats.shape[1]
     rows, width = w.shape
-    n = rows // blocks
+    n, half = rows // blocks, blocks // 2
     vmem = pl.BlockSpec(memory_space=pltpu.VMEM)
     return pl.pallas_call(
-        products_kernel,
-        out_shape=(pltpu.VMEM((2, blocks // 2, n, tokens), jnp.float32),) * 2,
-        in_specs=[pl.BlockSpec(memory_space=pltpu.SMEM), vmem, vmem, pl.BlockSpec(memory_space=pltpu.HBM)],
-        out_specs=(vmem, vmem),
-        scratch_shapes=[pltpu.VMEM((blocks, n, width), jnp.bfloat16), pltpu.SemaphoreType.DMA((blocks,))],
-        compiler_params=pltpu.CompilerParams(vmem_limit_bytes=VMEM - 16 * tokens * rows // 2 - 4 * tokens * width - (3 << 20)),
+        functools.partial(products_kernel, flip),
+        out_shape=pltpu.VMEM((2, half, n, tokens), jnp.float32),
+        in_specs=[vmem, vmem, pl.BlockSpec(memory_space=pltpu.HBM)],
+        out_specs=vmem,
+        scratch_shapes=[pltpu.VMEM((half, n, width), jnp.bfloat16), pltpu.SemaphoreType.DMA((half,))],
+        compiler_params=pltpu.CompilerParams(
+            vmem_limit_bytes=VMEM - 16 * tokens * rows // 2 - 4 * tokens * width - (3 << 20)
+        ),
         cost_estimate=pl.CostEstimate(
-            flops=4 * tokens * rows * width, bytes_accessed=2 * rows * width, transcendentals=0
+            flops=2 * tokens * rows * width, bytes_accessed=rows * width, transcendentals=0
         ),
-    )(low.reshape(1), stats, pltpu.with_memory_space_constraint(x, pltpu.VMEM), w)
+    )(
+        pltpu.with_memory_space_constraint(stats, pltpu.VMEM), pltpu.with_memory_space_constraint(x, pltpu.VMEM), w
+    )
 
 
 def swap(value, axis, size, mask):
@@ -129,7 +129,8 @@
         local, x = local_stats(grad_out, hidden_sum, norm_gain)
         stats = local[:2] + swap(local[:2], "tp", tp, lambda i: 1)
         local, x, stats = lax.optimization_barrier((local, x, stats))
-        give, keep = products(low, local, x, out_weight, tp)
+        give = products(1, local, x, out_weight, tp)
+        keep = products(0, local, x, out_weight, tp)
         for bit in range(1, count + 1):
             other = swap(stats, "tp", tp, lambda i: 1 << bit)
             stats = stats + other

time: 35.6 us -> 32.3 us (0.907)
  waiting for transfers between devices: 7.96 us -> 6.42 us
  starting transfers between devices: 13.5 us -> 12 us
  other arithmetic: 3.38 us -> 2.23 us
  Pallas kernels: 9.07 us -> 9.92 us
    ppermute x8, waiting for transfers between devices: 7.96 us -> 6.42 us  [swap(): return lax.ppermute(value, axis, [(i, i ^ mask(i)) for i in range(size)])]
    ppermute x8, starting transfers between devices: 13.5 us -> 12 us  [swap(): return lax.ppermute(value, axis, [(i, i ^ mask(i)) for i in range(size)])]
    reduce_sum x1, other arithmetic: 2.51 us -> 1.32 us  [body(): sums = jnp.sum(upstream * stream * inverse[:, None], axis=0)]
    pallas_call x1 -> x2, Pallas kernels: 7.36 us -> 8.21 us  [products(): pl.pallas_call(functools.partial(products_kernel, flip), out_shape=pltpu....]
    unnamed x5 -> x7, local copies, waits for them, and re-layouts: 0.75 us -> 0.75 us
  transfers between devices with their start and end apart: 8 -> 8, of which waited for: 5 -> 4; matrix products, arithmetic and copies ran while one was open for 9% -> 6% of each run, Pallas kernels for 0% -> 13%
where the time goes in v2:
time: 32.3 us; the launch traced here: 32.2 us
  starting transfers between devices  12 us (37%)
  Pallas kernels  9.92 us (31%)
  waiting for transfers between devices  6.42 us (20%)
  other arithmetic  2.23 us (7%)
  local copies, waits for them, and re-layouts  0.82 us (3%)
  between operations  0.76 us (2%)
    ppermute x8, starting transfers between devices, swap(): return lax.ppermute(value, axis, [(i, i ^ mask(i)) for i in range(size)])  12 us
    pallas_call x2, Pallas kernels, products(): pl.pallas_call(functools.partial(products_kernel, flip), out_shape=pltpu....  8.21 us
    ppermute x8, waiting for transfers between devices, swap(): return lax.ppermute(value, axis, [(i, i ^ mask(i)) for i in range(size)])  6.42 us
    pallas_call x1, Pallas kernels, local_stats(): pl.pallas_call(stats_kernel, out_shape=(pltpu.VMEM((3, tokens), jnp.float...  1.71 us
    reduce_sum x1, other arithmetic, body(): sums = jnp.sum(upstream * stream * inverse[:, None], axis=0)  1.32 us
    unnamed x7, local copies, waits for them, and re-layouts  0.75 us
  transfers between devices with their start and end apart: 8, of which 4 were waited for; matrix products, arithmetic and copies ran while one was open for 6% of the time, Pallas kernels for 13%

profile of v2, /device:TPU:0, one launch (start us, length us, event | category | flops | bytes accessed | tf_op | source)
XLA Modules:
  0.0 32.2 jit_solution(4916264795915117420)
XLA Ops:
  0.6 1.7 %shard_map.67 = (f32[3,128]{1,0:T(4,128)S(1)}, bf16[256,2048]{1,0:T(8,128)(2,1)S(1)}) custom-call(bf16[128,2048]{1,0:T(8,128)(2,1)} %go_hbm.1, bf16[128,2048]{1,0:T(8,128)(2,1)} %hs_hbm.1, f32[1,2048]{1,0:T(1,128)} %bitcast.25), custom_call_target="tpu_custom_call" | custom-call | flops 2097152 | bytes 1048576 | tf_op jit(solution)/shard_map/pallas_call | solution.py:48
  2.4 0.6 %collective-permute-start = (f32[2,128]{1,0:T(2,128)S(1)}, f32[2,128]{1,0:T(2,128)S(1)}, u32[]{:S(2)}, u32[]{:S(2)}) collective-permute-start(f32[2,128]{1,0:T(2,128)S(1)} %slice.16), channel_id=1, source_target_pairs={{0,4},{4,0},{8,12},{12,8},{16,20},{20,16},{24,28},{28,24},{1,5},{5... | collective-permute-start | bytes 3080 | tf_op jit(solution)/shard_map/ppermute | solution.py:116
  2.9 0.8 %collective-permute-done = f32[2,128]{1,0:T(2,128)S(1)} collective-permute-done((f32[2,128]{1,0:T(2,128)S(1)}, f32[2,128]{1,0:T(2,128)S(1)}, u32[]{:S(2)}, u32[]{:S(2)}) %collective-permute-start) | collective-permute-done | bytes 1056 | tf_op jit(solution)/shard_map/ppermute | solution.py:116
  3.7 4.1 %shard_map.69 = f32[2,4,256,128]{3,2,1,0:T(8,128)S(1)} custom-call(f32[3,128]{1,0:T(4,128)S(1)} %get-tuple-element.13.st_ref, bf16[256,2048]{1,0:T(8,128)(2,1)S(1)} %get-tuple-element.14.x, bf16[2048,2048]{1,0:T(8,128)(2,1)} %w_hbm.3), custom_call_target="tpu_custom_call" | custom-call | flops 1073741824 | bytes 4194304 | tf_op jit(solution)/shard_map/pallas_call | solution.py:98
  7.9 0.4 %collective-permute-start.3 = (f32[2,4,256,128]{3,2,1,0:T(8,128)S(1)}, f32[2,4,256,128]{3,2,1,0:T(8,128)S(1)}, u32[]{:S(2)}, u32[]{:S(2)}) collective-permute-start(f32[2,4,256,128]{3,2,1,0:T(8,128)S(1)} %shard_map.69), channel_id=1, source_target_pairs={{0,4},{4,0},{8,12},{12,8},{16,20},{20,16},{24,28},{28,24},{1,5},{5... | collective-permute-start | bytes 3145736 | tf_op jit(solution)/shard_map/ppermute | solution.py:116
  8.3 2.6 %collective-permute-start.1 = (f32[2,128]{1,0:T(2,128)S(1)}, f32[2,128]{1,0:T(2,128)S(1)}, u32[]{:S(2)}, u32[]{:S(2)}) collective-permute-start(f32[2,128]{1,0:T(2,128)S(1)} %slice_add_fusion), channel_id=1, source_target_pairs={{0,8},{4,12},{8,0},{12,4},{16,24},{20,28},{24,16},{28,20},{1,9},{5... | collective-permute-start | bytes 3080 | tf_op jit(solution)/shard_map/ppermute | solution.py:116
  10.9 1.6 %collective-permute-done.1 = f32[2,128]{1,0:T(2,128)S(1)} collective-permute-done((f32[2,128]{1,0:T(2,128)S(1)}, f32[2,128]{1,0:T(2,128)S(1)}, u32[]{:S(2)}, u32[]{:S(2)}) %collective-permute-start.1) | collective-permute-done | bytes 1056 | tf_op jit(solution)/shard_map/ppermute | solution.py:116
  12.5 0.0 copy-start
  12.5 0.0 copy-start.1
  12.5 0.0 copy-start.2
  12.5 2.1 %collective-permute-start.2 = (f32[2,128]{1,0:T(2,128)S(1)}, f32[2,128]{1,0:T(2,128)S(1)}, u32[]{:S(2)}, u32[]{:S(2)}) collective-permute-start(f32[2,128]{1,0:T(2,128)S(1)} %add.67), channel_id=1, source_target_pairs={{0,16},{4,20},{8,24},{12,28},{16,0},{20,4},{24,8},{28,12},{1,17},{... | collective-permute-start | bytes 3080 | tf_op jit(solution)/shard_map/ppermute | solution.py:116
  14.6 4.1 %shard_map.68 = f32[2,4,256,128]{3,2,1,0:T(8,128)S(1)} custom-call(f32[3,128]{1,0:T(4,128)S(1)} %get-tuple-element.13.st_ref, bf16[256,2048]{1,0:T(8,128)(2,1)S(1)} %get-tuple-element.14.x, bf16[2048,2048]{1,0:T(8,128)(2,1)} %w_hbm.3), custom_call_target="tpu_custom_call" | custom-call | flops 1073741824 | bytes 4194304 | tf_op jit(solution)/shard_map/pallas_call | solution.py:98
  18.7 0.0 collective-permute-done.2
  18.7 0.0 collective-permute-done.3
  18.8 0.1 add.71
  18.9 0.1 fusion.7
  19.1 1.6 %collective-permute-start.4 = (f32[2,256,128]{2,1,0:T(8,128)S(1)}, f32[2,256,128]{2,1,0:T(8,128)S(1)}, u32[]{:S(2)}, u32[]{:S(2)}) collective-permute-start(f32[2,256,128]{2,1,0:T(8,128)S(1)} %pad_maximum_fusion), channel_id=1, source_target_pairs={{0,8},{4,20},{8,0},{12,28},{16,24},{20,4},{24,16},{28,12},{1,9},{5... | collective-permute-start | bytes 786440 | tf_op jit(solution)/shard_map/ppermute | solution.py:116
  20.6 0.0 copy-done
  20.6 0.0 copy-done.1
  20.6 0.0 copy-done.2
  20.6 1.3 %fusion.4 = (f32[2048]{0:T(1024)S(1)}, bf16[128,2048]{1,0:T(8,128)(2,1)}) fusion(bf16[128,2048]{1,0:T(8,128)(2,1)S(1)} %copy-done, bf16[128,2048]{1,0:T(8,128)(2,1)S(1)} %copy-done.1, f32[128]{0:T(128)S(1)} %rsqrt_bitcast_fusion, f32[128]{0:T(128)S(1)} %fusion.9, f32[2048]{0:T(1024)S(1)} %copy-done.2), kind=kLoop, calls=%fused_computation.7 | loop fusion | flops 2619392 | bytes 1590272 | tf_op jit(solution)/shard_map/reduce_sum | solution.py:179
  21.9 1.6 %collective-permute-start.5 = (f32[2048]{0:T(1024)S(1)}, f32[2048]{0:T(1024)S(1)}, u32[]{:S(2)}, u32[]{:S(2)}) collective-permute-start(f32[2048]{0:T(1024)S(1)} %get-tuple-element.20), channel_id=1, source_target_pairs={{0,1},{1,0},{2,3},{3,2},{4,5},{5,4},{6,7},{7,6},{8,9},{9,8},{10,11... | collective-permute-start | bytes 24584 | tf_op jit(solution)/shard_map/ppermute | solution.py:116
  23.5 2.1 %collective-permute-done.5 = f32[2048]{0:T(1024)S(1)} collective-permute-done((f32[2048]{0:T(1024)S(1)}, f32[2048]{0:T(1024)S(1)}, u32[]{:S(2)}, u32[]{:S(2)}) %collective-permute-start.5) | collective-permute-done | bytes 8224 | tf_op jit(solution)/shard_map/ppermute | solution.py:116
  25.6 0.0 collective-permute-done.4
  25.7 0.6 %collective-permute-start.6 = (f32[1,256,128]{2,1,0:T(8,128)S(1)}, f32[1,256,128]{2,1,0:T(8,128)S(1)}, u32[]{:S(2)}, u32[]{:S(2)}) collective-permute-start(f32[1,256,128]{2,1,0:T(8,128)S(1)} %constant_dynamic-slice_fusion), channel_id=1, source_target_pairs={{0,16},{4,12},{8,24},{12,4},{16,0},{20,28},{24,8},{28,20},{1,17},{... | collective-permute-start | bytes 393224 | tf_op jit(solution)/shard_map/ppermute | solution.py:116
  26.2 2.6 %collective-permute-start.7 = (f32[2048]{0:T(1024)S(1)}, f32[2048]{0:T(1024)S(1)}, u32[]{:S(2)}, u32[]{:S(2)}) collective-permute-start(f32[2048]{0:T(1024)S(1)} %add.79), channel_id=1, source_target_pairs={{0,2},{1,3},{2,0},{3,1},{4,6},{5,7},{6,4},{7,5},{8,10},{9,11},{10,... | collective-permute-start | bytes 24584 | tf_op jit(solution)/shard_map/ppermute | solution.py:116
  28.8 2.0 %collective-permute-done.7 = f32[2048]{0:T(1024)S(1)} collective-permute-done((f32[2048]{0:T(1024)S(1)}, f32[2048]{0:T(1024)S(1)}, u32[]{:S(2)}, u32[]{:S(2)}) %collective-permute-start.7) | collective-permute-done | bytes 8224 | tf_op jit(solution)/shard_map/ppermute | solution.py:116
  30.8 0.6 %add.81 = f32[2048]{0:T(1024)} add(f32[2048]{0:T(1024)S(1)} %add.79, f32[2048]{0:T(1024)S(1)} %collective-permute-done.7) | non-fusion elementwise | flops 2048 | bytes 24576 | tf_op jit(solution)/shard_map/add | solution.py:186
  31.4 0.0 collective-permute-done.6
  31.4 0.7 %copy.7 = bf16[128,256]{1,0:T(8,128)(2,1)} copy(bf16[128,256]{0,1:T(8,128)(2,1)S(1)} %fusion.8) | data formatting | bytes 131072
  (12 shorter events, 0.2 us)
Async XLA Ops:
  2.4 1.4 %collective-permute-start = (f32[2,128]{1,0:T(2,128)S(1)}, f32[2,128]{1,0:T(2,128)S(1)}, u32[]{:S(2)}, u32[]{:S(2)}) collective-permute-start(f32[2,128]{1,0:T(2,128)S(1)} %slice.16), channel_id=1, source_target_pairs={{0,4},{4,0},{8,12},{12,8},{16,20},{20,16},{24,28},{28,24},{1,5},{5... | collective-permute-start | bytes 3080 | tf_op jit(solution)/shard_map/ppermute | solution.py:116
  7.9 10.9 %collective-permute-start.3 = (f32[2,4,256,128]{3,2,1,0:T(8,128)S(1)}, f32[2,4,256,128]{3,2,1,0:T(8,128)S(1)}, u32[]{:S(2)}, u32[]{:S(2)}) collective-permute-start(f32[2,4,256,128]{3,2,1,0:T(8,128)S(1)} %shard_map.69), channel_id=1, source_target_pairs={{0,4},{4,0},{8,12},{12,8},{16,20},{20,16},{24,28},{28,24},{1,5},{5... | collective-permute-start | bytes 3145736 | tf_op jit(solution)/shard_map/ppermute | solution.py:116
  8.3 4.2 %collective-permute-start.1 = (f32[2,128]{1,0:T(2,128)S(1)}, f32[2,128]{1,0:T(2,128)S(1)}, u32[]{:S(2)}, u32[]{:S(2)}) collective-permute-start(f32[2,128]{1,0:T(2,128)S(1)} %slice_add_fusion), channel_id=1, source_target_pairs={{0,8},{4,12},{8,0},{12,4},{16,24},{20,28},{24,16},{28,20},{1,9},{5... | collective-permute-start | bytes 3080 | tf_op jit(solution)/shard_map/ppermute | solution.py:116
  12.5 8.2 %copy-start = (bf16[128,2048]{1,0:T(8,128)(2,1)S(1)}, bf16[128,2048]{1,0:T(8,128)(2,1)}, u32[]{:S(2)}) copy-start(bf16[128,2048]{1,0:T(8,128)(2,1)} %hs_hbm.1) | copy-start | bytes 1572868
  12.5 8.2 %copy-start.1 = (bf16[128,2048]{1,0:T(8,128)(2,1)S(1)}, bf16[128,2048]{1,0:T(8,128)(2,1)}, u32[]{:S(2)}) copy-start(bf16[128,2048]{1,0:T(8,128)(2,1)} %go_hbm.1) | copy-start | bytes 1572868
  12.5 8.2 %copy-start.2 = (f32[2048]{0:T(1024)S(1)}, f32[2048]{0:T(1024)}, u32[]{:S(2)}) copy-start(f32[2048]{0:T(1024)} %param.6) | copy-start | bytes 24580
  12.5 6.2 %collective-permute-start.2 = (f32[2,128]{1,0:T(2,128)S(1)}, f32[2,128]{1,0:T(2,128)S(1)}, u32[]{:S(2)}, u32[]{:S(2)}) collective-permute-start(f32[2,128]{1,0:T(2,128)S(1)} %add.67), channel_id=1, source_target_pairs={{0,16},{4,20},{8,24},{12,28},{16,0},{20,4},{24,8},{28,12},{1,17},{... | collective-permute-start | bytes 3080 | tf_op jit(solution)/shard_map/ppermute | solution.py:116
  19.1 6.5 %collective-permute-start.4 = (f32[2,256,128]{2,1,0:T(8,128)S(1)}, f32[2,256,128]{2,1,0:T(8,128)S(1)}, u32[]{:S(2)}, u32[]{:S(2)}) collective-permute-start(f32[2,256,128]{2,1,0:T(8,128)S(1)} %pad_maximum_fusion), channel_id=1, source_target_pairs={{0,8},{4,20},{8,0},{12,28},{16,24},{20,4},{24,16},{28,12},{1,9},{5... | collective-permute-start | bytes 786440 | tf_op jit(solution)/shard_map/ppermute | solution.py:116
  21.9 3.7 %collective-permute-start.5 = (f32[2048]{0:T(1024)S(1)}, f32[2048]{0:T(1024)S(1)}, u32[]{:S(2)}, u32[]{:S(2)}) collective-permute-start(f32[2048]{0:T(1024)S(1)} %get-tuple-element.20), channel_id=1, source_target_pairs={{0,1},{1,0},{2,3},{3,2},{4,5},{5,4},{6,7},{7,6},{8,9},{9,8},{10,11... | collective-permute-start | bytes 24584 | tf_op jit(solution)/shard_map/ppermute | solution.py:116
  25.7 5.7 %collective-permute-start.6 = (f32[1,256,128]{2,1,0:T(8,128)S(1)}, f32[1,256,128]{2,1,0:T(8,128)S(1)}, u32[]{:S(2)}, u32[]{:S(2)}) collective-permute-start(f32[1,256,128]{2,1,0:T(8,128)S(1)} %constant_dynamic-slice_fusion), channel_id=1, source_target_pairs={{0,16},{4,12},{8,24},{12,4},{16,0},{20,28},{24,8},{28,20},{1,17},{... | collective-permute-start | bytes 393224 | tf_op jit(solution)/shard_map/ppermute | solution.py:116
  26.2 4.5 %collective-permute-start.7 = (f32[2048]{0:T(1024)S(1)}, f32[2048]{0:T(1024)S(1)}, u32[]{:S(2)}, u32[]{:S(2)}) collective-permute-start(f32[2048]{0:T(1024)S(1)} %add.79), channel_id=1, source_target_pairs={{0,2},{1,3},{2,0},{3,1},{4,6},{5,7},{6,4},{7,5},{8,10},{9,11},{10,... | collective-permute-start | bytes 24584 | tf_op jit(solution)/shard_map/ppermute | solution.py:116
